TPU v7x, 512 devices: a 8x2x16 block of a 8x16x16 slice. The times are simulated.
512 devices in a mesh: job: 2 (over y), ta: 16 (over z), xyz: 8 (over x), src: 2 (over core).
Axes of the slice: x: 8, y: 2, z: 16, core: 2. Of those that a mesh axis runs over, the one named last changes fastest.
The devices are a block of a 8x16x16 slice.
Arguments:
- spinors: float32 [64, 32, 2, 8, 3, 2048], P('src', 'ta', None, 'job', None, 'xyz'), parts along dimension 3, may hold values from -6 to 6
- eigvecs: float32 [32, 256, 2, 3, 2048], P('ta', 'job', None, None, 'xyz'), parts along dimension 1, may hold values from -0.0546875 to 0.0546875
- group_of: int32 [32], replicated, may hold values from 0 to 15, as said below
- source_ids: int32 [64], P('src'), may hold values from 0 to 63, as said below
Outputs:
- perambulator: float32 [32, 2, 8, 64, 128], P('ta', None, 'job', 'src', 'xyz'), parts along dimension 2
There are 2 independent parts, one for each index of `job`. A program takes and returns all parts, laid end to end along the dimension named above; an argument that names none is the same for every part. Nothing has to cross between parts.
Inputs may be any that keep to these rules, and one draw needn't show every extreme that they name: `group_of`: every group number appears exactly 2 times. `source_ids`: the 32 entries held by index i of src are a permutation of i * 32 to (i + 1) * 32 - 1.
All inputs are finite; a program needn't handle non-finite values.
Results may differ from a plain program's by a relative error of at most 0.00007.
Values sent between devices are 32-bit elements; how exact they have to be, the bound alone decides.
A program may use at most 64 MiB of HBM per device.

v0:
```python
import jax
import jax.numpy as jnp
from jax import lax
from jax.sharding import PartitionSpec as P


def in_blocks(x, dim, size):
    dims = x.shape
    pieces = x.reshape(*dims[:dim], size, dims[dim] // size, *dims[dim + 1 :])
    return jnp.moveaxis(pieces, dim, 0)


def sent_and_summed(x, axis, dim):
    size = lax.axis_size(axis)
    pieces = lax.all_to_all(in_blocks(x, dim, size), axis, 0, 0, tiled=True)
    return jnp.sum(pieces, axis=0)


def contract_pair(vectors, spinor):
    vector_real = vectors[:, :, 0]
    vector_imag = vectors[:, :, 1]
    spinor_real = spinor[:, :, 0]
    spinor_imag = spinor[:, :, 1]

    def contract(left_side, right_side):
        return jnp.einsum(
            "tkcx,ntscx->tsnk", left_side, right_side, precision=lax.Precision.HIGHEST
        )

    real_part = contract(vector_real, spinor_real) + contract(vector_imag, spinor_imag)
    imag_part = contract(vector_real, spinor_imag) - contract(vector_imag, spinor_real)
    return jnp.stack([real_part, imag_part], axis=1)


def local(spinors, eigvecs, group_of, source_ids):
    extent = group_of.shape[0]
    sort_keys = group_of * extent + jnp.arange(extent, dtype=jnp.int32)
    ordering = jnp.argsort(sort_keys)
    spread = lax.all_to_all(spinors, "ta", split_axis=0, concat_axis=1, tiled=True)
    grouped = jnp.take(spread, ordering, axis=1)
    regrouped = lax.all_to_all(grouped, "ta", split_axis=1, concat_axis=0, tiled=True)
    partial_sums = contract_pair(eigvecs, regrouped)
    summed = sent_and_summed(partial_sums, "xyz", 4)
    inverse = jnp.argsort(source_ids)
    return jnp.take(summed, inverse, axis=3)


def solution(mesh):
    in_specs = (
        P("src", "ta", None, "job", None, "xyz"),
        P("ta", "job", None, None, "xyz"),
        P(),
        P("src"),
    )
    out_specs = P("ta", None, "job", "src", "xyz")
    return jax.shard_map(local, mesh=mesh, in_specs=in_specs, out_specs=out_specs, check_vma=False)
```

profile of v0, /device:TPU:80, one launch (start us, length us, event | category | flops | bytes accessed | tf_op | source)
XLA Modules:
  0.0 233.5 jit_solution(13181395401285672478)
XLA Ops:
  0.0 0.0 copy-start
  0.0 43.9 %all-to-all-start = ((f32[32,2,2,4,3,256]{5,3,4,2,1,0:T(4,128)}), f32[32,2,2,4,3,256]{5,3,4,2,1,0:T(4,128)S(1)}, u32[]{:S(2)}, u32[]{:S(2)}) async-start(f32[32,2,2,4,3,256]{5,3,4,2,1,0:T(4,128)} %param.4), calls=%async_computation | async-start | bytes 3145728 | tf_op jit(solution)/shard_map/all_to_all | solution.py:39
  43.9 0.0 copy-done
  43.9 1.6 sort.32
  45.5 72.4 %all-to-all-done = f32[32,2,2,4,3,256]{5,3,4,2,1,0:T(4,128)S(1)} async-done(((f32[32,2,2,4,3,256]{5,3,4,2,1,0:T(4,128)}), f32[32,2,2,4,3,256]{5,3,4,2,1,0:T(4,128)S(1)}, u32[]{:S(2)}, u32[]{:S(2)}) %all-to-all-start) | async-done | bytes 1572896 | tf_op jit(solution)/shard_map/all_to_all | solution.py:39
  117.9 0.3 copy.15
  118.2 1.5 gather_fusion
  119.7 1.6 select_bitcast_fusion
  121.4 0.0 copy-start.1
  121.4 6.4 %all-to-all-start.1 = ((f32[2,32,2,4,3,256]{5,3,4,2,0,1:T(4,128)}), f32[2,32,2,4,3,256]{5,3,4,2,0,1:T(4,128)S(1)}, u32[]{:S(2)}, u32[]{:S(2)}) async-start(f32[2,32,2,4,3,256]{5,3,4,2,0,1:T(4,128)} %select_bitcast_fusion), calls=%async_computation.1 | async-start | bytes 3145728 | tf_op jit(solution)/shard_map/all_to_all | solution.py:41
  127.8 0.0 copy-done.1
  127.8 1.6 sort.31
  129.4 3.4 %fusion.4 = (f32[2,128,1,3,256]{4,2,3,1,0:T(1,128)S(1)}, f32[2,128,1,3,256]{4,2,3,1,0:T(1,128)S(1)}) fusion(f32[2,128,2,3,256]{4,2,3,1,0:T(2,128)} %param.5), kind=kLoop, calls=%fused_computation.24 | loop fusion | bytes 3145728 | tf_op jit(solution)/shard_map/slice | solution.py:20
  132.8 69.2 %all-to-all-done.1 = f32[2,32,2,4,3,256]{5,3,4,2,0,1:T(4,128)S(1)} async-done(((f32[2,32,2,4,3,256]{5,3,4,2,0,1:T(4,128)}), f32[2,32,2,4,3,256]{5,3,4,2,0,1:T(4,128)S(1)}, u32[]{:S(2)}, u32[]{:S(2)}) %all-to-all-start.1) | async-done | bytes 1572896 | tf_op jit(solution)/shard_map/all_to_all | solution.py:41
  202.0 2.0 copy.17
  204.0 2.4 %all_to_all.36 = f32[32,2,2,4,3,256]{5,0,4,3,1,2:T(8,128)S(1)} reshape(f32[16,2,2,2,4,3,256]{6,1,0,5,4,2,3:T(2,128)} %copy.17) | data formatting | bytes 3145728 | tf_op jit(solution)/shard_map/all_to_all | solution.py:41
  206.4 0.9 convolution_bitcast_fusion
  207.2 0.9 convolution_bitcast_fusion.2
  208.1 0.9 fusion.1
  209.0 0.9 fusion.3
  209.9 0.2 copy.21
  210.1 0.2 copy.20
  210.3 0.1 copy_bitcast_fusion.6
  210.5 1.2 reshape.39
  211.6 7.3 %all-to-all-start.2 = ((f32[8,1,8192]{2,1,0:T(1,128)}), f32[8,1,8192]{2,1,0:T(1,128)S(1)}, u32[]{:S(2)}, u32[]{:S(2)}) async-start(f32[8,1,8192]{2,1,0:T(1,128)} %reshape.39), calls=%async_computation.2 | async-start | bytes 524288 | tf_op jit(solution)/shard_map/all_to_all | solution.py:15
  219.0 10.4 %all-to-all-done.2 = f32[8,1,8192]{2,1,0:T(1,128)S(1)} async-done(((f32[8,1,8192]{2,1,0:T(1,128)}), f32[8,1,8192]{2,1,0:T(1,128)S(1)}, u32[]{:S(2)}, u32[]{:S(2)}) %all-to-all-start.2) | async-done | bytes 262176 | tf_op jit(solution)/shard_map/all_to_all | solution.py:15
  229.4 0.5 broadcast.24
  229.9 1.3 reduce
  231.2 0.3 reshape.40
  231.5 0.1 bitcast_reduce_fusion
  231.6 0.1 copy.24
  231.8 0.7 gather_fusion.1
  232.5 0.1 select_bitcast_fusion.1
  232.7 0.8 copy.25
  (9 shorter events, 0.0 us)
Async XLA Ops:
  0.0 43.9 %copy-start = (s32[32]{0:T(128)S(1)}, s32[32]{0:T(128)}, u32[]{:S(2)}) copy-start(s32[32]{0:T(128)} %param.6) | copy-start | bytes 388
  0.0 117.9 %all-to-all-start = ((f32[32,2,2,4,3,256]{5,3,4,2,1,0:T(4,128)}), f32[32,2,2,4,3,256]{5,3,4,2,1,0:T(4,128)S(1)}, u32[]{:S(2)}, u32[]{:S(2)}) async-start(f32[32,2,2,4,3,256]{5,3,4,2,1,0:T(4,128)} %param.4), calls=%async_computation | async-start | bytes 3145728 | tf_op jit(solution)/shard_map/all_to_all | solution.py:39
  121.4 6.5 %copy-start.1 = (s32[32]{0:T(128)S(1)}, s32[32]{0:T(128)}, u32[]{:S(2)}) copy-start(s32[32]{0:T(128)} %param.7) | copy-start | bytes 388
  121.4 80.7 %all-to-all-start.1 = ((f32[2,32,2,4,3,256]{5,3,4,2,0,1:T(4,128)}), f32[2,32,2,4,3,256]{5,3,4,2,0,1:T(4,128)S(1)}, u32[]{:S(2)}, u32[]{:S(2)}) async-start(f32[2,32,2,4,3,256]{5,3,4,2,0,1:T(4,128)} %select_bitcast_fusion), calls=%async_computation.1 | async-start | bytes 3145728 | tf_op jit(solution)/shard_map/all_to_all | solution.py:41
  211.6 17.8 %all-to-all-start.2 = ((f32[8,1,8192]{2,1,0:T(1,128)}), f32[8,1,8192]{2,1,0:T(1,128)S(1)}, u32[]{:S(2)}, u32[]{:S(2)}) async-start(f32[8,1,8192]{2,1,0:T(1,128)} %reshape.39), calls=%async_computation.2 | async-start | bytes 524288 | tf_op jit(solution)/shard_map/all_to_all | solution.py:15
where the time goes:
time: 234 us; the launch traced here: 233 us
  waiting for transfers between devices  152 us (65%)
  starting transfers between devices  57.6 us (25%)
  local copies, waits for them, and re-layouts  13.6 us (6%)
  other arithmetic  6.47 us (3%)
  matrix products  3.51 us (2%)
    all_to_all x1, waiting for transfers between devices, local(): lax.all_to_all(spinors, 'ta', split_axis=0, concat_axis=1, tiled=True)  72.4 us
    all_to_all x1, waiting for transfers between devices, local(): lax.all_to_all(grouped, 'ta', split_axis=1, concat_axis=0, tiled=True)  69.2 us
    all_to_all x1, starting transfers between devices, local(): lax.all_to_all(spinors, 'ta', split_axis=0, concat_axis=1, tiled=True)  43.9 us
    all_to_all x1, waiting for transfers between devices, sent_and_summed(): pieces = lax.all_to_all(in_blocks(x, dim, size), axis, 0, 0, tiled=True)  10.4 us
    all_to_all x1, starting transfers between devices, sent_and_summed(): pieces = lax.all_to_all(in_blocks(x, dim, size), axis, 0, 0, tiled=True)  7.32 us
    all_to_all x1, starting transfers between devices, local(): lax.all_to_all(grouped, 'ta', split_axis=1, concat_axis=0, tiled=True)  6.44 us
  transfers between devices with their start and end apart: 3, of which 3 were waited for; matrix products, arithmetic and copies ran while one was open for 3% of the time, Pallas kernels for 0%

commit v1 on v0

v1 whole, which is shorter than its diff:
```python
import functools

import jax
import jax.numpy as jnp
from jax import lax
from jax.experimental import pallas as pl
from jax.experimental.pallas import tpu as pltpu
from jax.sharding import PartitionSpec as P

MESH = pl.DeviceIdType.MESH
LANES = 128
Q = 2


def kernel(sizes, group_ref, ids_ref, vec_ref, spin_ref, out_ref,
           rank, order, inverse, raw, both, high, low, mids, mail, gathered, left,
           part, parts, home, relay, post, back,
           load_sem, own_sem, pair_sem, s1, r1, s2, r2, s3, r3, s4, r4, s5, r5):
    nz, nx, nc, ns, nt, spin, depth, keep = sizes
    z, x, c = lax.axis_index("ta"), lax.axis_index("xyz"), lax.axis_index("src")
    other = 1 - c
    rows = ns * spin
    chunk = keep * depth
    half = nx // nc

    def far(d):
        return lax.rem(z + d, nz)

    barrier = pltpu.get_barrier_semaphore()

    @pl.loop(1, nz)
    def _(d):
        pl.semaphore_signal(barrier, inc=1, device_id={"ta": far(d)}, device_id_type=MESH)

    @pl.loop(1, nx)
    def _(d):
        there = lax.rem(x + d, nx)
        for core in range(nc):
            pl.semaphore_signal(barrier, inc=1, device_id={"xyz": there, "src": core}, device_id_type=MESH)

    pl.semaphore_signal(barrier, inc=1, device_id={"src": other}, device_id_type=MESH)

    load = pltpu.make_async_copy(spin_ref, raw, load_sem)
    load.start()
    pl.semaphore_wait(barrier, (nz - 1) + (nx - 1) * nc + 1)

    def share(q, there):
        first = (c * (nz * Q * keep) + there * (Q * keep) + q * keep) * depth
        return vec_ref.at[:, pl.ds(pl.multiple_of(first, 8), chunk), :]

    def spread(q, d):
        return pltpu.make_async_remote_copy(
            src_ref=share(q, far(d)), dst_ref=mids[q].at[pl.ds(nt * z, nt)],
            send_sem=s1.at[q, d], recv_sem=r1.at[q, d], device_id={"ta": far(d)}, device_id_type=MESH)

    def deliver(q, d):
        return pltpu.make_async_remote_copy(
            src_ref=mail.at[q, d], dst_ref=gathered.at[q, :, pl.ds(pl.multiple_of(z * chunk, 8), chunk), :],
            send_sem=s2.at[q, d], recv_sem=r2.at[q, d], device_id={"ta": far(d)}, device_id_type=MESH)

    for q in range(Q):
        @pl.loop(1, nz)
        def _(d):
            spread(q, d).start()

        pltpu.make_async_copy(share(q, z), mids[q].at[pl.ds(nt * z, nt)], own_sem.at[q]).start()

    count = nz * nt

    @pl.loop(0, count)
    def _(t):
        mine = group_ref[t] * count + t
        total = jnp.int32(0)
        for u in range(count):
            total += jnp.where(group_ref[u] * count + u < mine, 1, 0)
        rank[t] = total

    @pl.loop(0, count)
    def _(r):
        total = jnp.int32(0)
        for u in range(count):
            total = jnp.maximum(total, jnp.where(rank[u] == r, u, 0))
        order[r] = total

    @pl.loop(0, ns)
    def _(j):
        total = jnp.int32(0)
        for u in range(ns):
            total = jnp.maximum(total, jnp.where(ids_ref[u] - c * ns == j, u, 0))
        inverse[j] = total

    load.wait()

    @pl.loop(0, ns)
    def _(j):
        n = inverse[j]
        for tl in range(nt):
            for g in range(depth):
                for s in range(spin):
                    both[c, tl, g, pl.ds(s * ns + j, 1), :] = raw[n, tl, g * spin + s:g * spin + s + 1, :]

    pair = pltpu.make_async_remote_copy(
        src_ref=both.at[c], dst_ref=both.at[c], send_sem=pair_sem.at[0], recv_sem=pair_sem.at[1],
        device_id={"src": other}, device_id_type=MESH)
    pair.start()
    pair.wait()

    @pl.loop(0, nt)
    def _(tl):
        for core in range(nc):
            for g in range(depth):
                block = both[core, tl, g]
                top = block.astype(jnp.bfloat16)
                high[tl, core * rows:(core + 1) * rows, g * LANES:(g + 1) * LANES] = top
                low[tl, core * rows:(core + 1) * rows, g * LANES:(g + 1) * LANES] = (block - top.astype(jnp.float32)).astype(jnp.bfloat16)

    for q in range(Q):
        @pl.loop(1, nz)
        def _(d):
            spread(q, d).wait_recv()

        pltpu.make_async_copy(share(q, z), mids[q].at[pl.ds(nt * z, nt)], own_sem.at[q]).wait()

        @pl.loop(1, nz)
        def _(d):
            for tl in range(nt):
                mail[q, d, tl] = mids[q][rank[nt * far(d) + tl]]

        for tl in range(nt):
            gathered[q, tl, pl.ds(pl.multiple_of(z * chunk, 8), chunk), :] = mids[q][rank[nt * z + tl]]

        @pl.loop(1, nz)
        def _(d):
            deliver(q, d).start()

    contract = (((1,), (1,)), ((), ()))
    ks = nz * keep
    colours = depth // 4

    def reduce_copy(q, xs, core):
        return pltpu.make_async_remote_copy(
            src_ref=part.at[q, xs, core], dst_ref=parts.at[q, x],
            send_sem=s3.at[q, xs, core], recv_sem=r3.at[q, x],
            device_id={"xyz": half * c + xs, "src": core}, device_id_type=MESH)

    sender = lax.div(x, half)
    for q in range(Q):
        @pl.loop(1, nz)
        def _(d):
            deliver(q, d).wait_recv()

        for tl in range(nt):
            for i in range(colours):
                for b in range(2):
                    re = gathered[q, tl, pl.ds(i * 4 + b * 2, ks, stride=depth), :]
                    im = gathered[q, tl, pl.ds(i * 4 + b * 2 + 1, ks, stride=depth), :]
                    g = i * 2 + b
                    for at, value in ((0, re), (depth // 2, im)):
                        top = value.astype(jnp.bfloat16)
                        rest = (value - top.astype(jnp.float32)).astype(jnp.bfloat16)
                        where = slice((at + g) * LANES, (at + g + 1) * LANES)
                        cross = slice((depth // 2 - at + g) * LANES, (depth // 2 - at + g + 1) * LANES)
                        left[0:ks, where] = top
                        left[2 * ks:3 * ks, where] = rest
                        left[ks:2 * ks, cross] = top if at == 0 else -top
                        left[3 * ks:4 * ks, cross] = rest if at == 0 else -rest
            one = lax.dot_general(left[...], high[tl], contract, preferred_element_type=jnp.float32)
            two = lax.dot_general(left[0:2 * ks, :], low[tl], contract, preferred_element_type=jnp.float32)
            total = one[0:2 * ks] + one[2 * ks:4 * ks] + two
            step = ks // half
            for xs in range(half):
                for core in range(nc):
                    for reim in range(2):
                        part[q, xs, core, tl, reim] = total[reim * ks + xs * step:reim * ks + (xs + 1) * step, core * rows:(core + 1) * rows]

        for xs in range(half):
            for core in range(nc):
                mine = jnp.logical_and(half * c + xs == x, c == core)

                @pl.when(jnp.logical_not(mine))
                def _():
                    reduce_copy(q, xs, core).start()

                @pl.when(mine)
                def _():
                    parts[q, x] = part[q, xs, core]

    def return_copy(d):
        return pltpu.make_async_remote_copy(
            src_ref=home.at[far(d)], dst_ref=relay.at[pl.ds(nt * z, nt)],
            send_sem=s4.at[d], recv_sem=r4.at[d], device_id={"ta": far(d)}, device_id_type=MESH)

    def final_copy(d):
        return pltpu.make_async_remote_copy(
            src_ref=post.at[far(d)], dst_ref=back.at[z],
            send_sem=s5.at[d], recv_sem=r5.at[d], device_id={"ta": far(d)}, device_id_type=MESH)

    per = nz // (Q * 2)
    for q in range(Q):
        for xs in range(nx):
            @pl.when(jnp.logical_not(jnp.logical_and(xs == x, sender == c)))
            def _():
                pltpu.make_async_remote_copy(
                    src_ref=part.at[q, 0, 0], dst_ref=parts.at[q, xs], send_sem=s3.at[q, 0, 0], recv_sem=r3.at[q, xs],
                    device_id={"src": other}, device_id_type=MESH).wait_recv()

        for tl in range(nt):
            for reim in range(2):
                total = parts[q, 0, tl, reim]
                for xs in range(1, nx):
                    total += parts[q, xs, tl, reim]
                for i in range(per):
                    home[(q * 2 + reim) * per + i, tl] = total[i * keep:(i + 1) * keep, :]

    @pl.loop(1, nz)
    def _(d):
        return_copy(d).start()

    for tl in range(nt):
        relay[nt * z + tl] = home[z, tl]

    @pl.loop(1, nz)
    def _(d):
        return_copy(d).wait_recv()

    @pl.loop(0, nz)
    def _(there):
        for tl in range(nt):
            post[there, tl] = relay[order[nt * there + tl]]

    @pl.loop(1, nz)
    def _(d):
        final_copy(d).start()

    back[z] = post[z]

    @pl.loop(1, nz)
    def _(d):
        final_copy(d).wait_recv()

    for q in range(Q):
        for reim in range(2):
            for i in range(per):
                for tl in range(nt):
                    at = i * Q * keep + q * keep
                    out_ref[tl, reim, at:at + keep, :] = back[(q * 2 + reim) * per + i, tl]

    for q in range(Q):
        @pl.loop(1, nz)
        def _(d):
            spread(q, d).wait_send()
            deliver(q, d).wait_send()

        for xs in range(half):
            for core in range(nc):
                @pl.when(jnp.logical_not(jnp.logical_and(half * c + xs == x, c == core)))
                def _():
                    reduce_copy(q, xs, core).wait_send()

    @pl.loop(1, nz)
    def _(d):
        return_copy(d).wait_send()
        final_copy(d).wait_send()


def solution(mesh):
    nz, nx, nc = mesh.shape["ta"], mesh.shape["xyz"], mesh.shape["src"]

    def local(spinors, eigvecs, group_of, source_ids):
        ns, nt, _, spin, colours, sites = spinors.shape
        kk = eigvecs.shape[1]
        blocks = sites // LANES
        depth = 2 * colours * blocks
        keep = kk // (nc * nz * Q)
        rows = ns * spin
        ks = nz * keep
        spin_view = spinors.transpose(0, 1, 2, 4, 3, 5).reshape(ns, nt, 2, colours, spin, blocks, LANES)
        spin_view = spin_view.transpose(0, 1, 2, 3, 5, 4, 6).reshape(ns, nt, depth * spin, LANES)
        vec_view = eigvecs.transpose(0, 1, 3, 2, 4).reshape(nt, kk, colours, 2, blocks, LANES)
        vec_view = vec_view.transpose(0, 1, 2, 4, 3, 5).reshape(nt, kk * depth, LANES)
        sizes = (nz, nx, nc, ns, nt, spin, depth, keep)
        f32, bf16 = jnp.float32, jnp.bfloat16
        dma = pltpu.SemaphoreType.DMA
        small = (keep, LANES)
        flat = pl.pallas_call(
            functools.partial(kernel, sizes),
            out_shape=jax.ShapeDtypeStruct((nt, 2, kk // nx, rows), f32),
            in_specs=[pl.BlockSpec(memory_space=pltpu.SMEM)] * 2 + [pl.BlockSpec(memory_space=pl.ANY)] * 2,
            out_specs=pl.BlockSpec(memory_space=pltpu.VMEM),
            scratch_shapes=[
                pltpu.SMEM((nz * nt,), jnp.int32),
                pltpu.SMEM((nz * nt,), jnp.int32),
                pltpu.SMEM((ns,), jnp.int32),
                pltpu.VMEM((ns, nt, depth * spin, LANES), f32),
                pltpu.VMEM((nc, nt, depth, rows, LANES), f32),
                pltpu.VMEM((nt, nc * rows, depth * LANES), bf16),
                pltpu.VMEM((nt, nc * rows, depth * LANES), bf16),
                [pltpu.VMEM((nz * nt, keep * depth, LANES), f32)] * Q,
                pltpu.VMEM((Q, nz, nt, keep * depth, LANES), f32),
                pltpu.VMEM((Q, nt, ks * depth, LANES), f32),
                pltpu.VMEM((4 * ks, depth * LANES), bf16),
                pltpu.VMEM((Q, nx // nc, nc, nt, 2, ks * nc // nx, LANES), f32),
                pltpu.VMEM((Q, nx, nt, 2, ks * nc // nx, LANES), f32),
                pltpu.VMEM((nz, nt) + small, f32),
                pltpu.VMEM((nz * nt,) + small, f32),
                pltpu.VMEM((nz, nt) + small, f32),
                pltpu.VMEM((nz, nt) + small, f32),
                dma, dma((Q,)), dma((2,)),
                dma((Q, nz)), dma((Q, nz)), dma((Q, nz)), dma((Q, nz)),
                dma((Q, nx // nc, nc)), dma((Q, nx)),
                dma((nz,)), dma((nz,)), dma((nz,)), dma((nz,)),
            ],
            compiler_params=pltpu.CompilerParams(collective_id=0, has_side_effects=True),
        )(group_of, source_ids, vec_view, spin_view)
        return flat.reshape(nt, 2, kk // nx, spin, ns).transpose(0, 1, 3, 4, 2)

    in_specs = (
        P("src", "ta", None, "job", None, "xyz"),
        P("ta", "job", None, None, "xyz"),
        P(),
        P("src"),
    )
    out_specs = P("ta", None, "job", "src", "xyz")
    return jax.shard_map(local, mesh=mesh, in_specs=in_specs, out_specs=out_specs, check_vma=False)
```

time: 234 us -> 148 us (0.63)
  waiting for transfers between devices: 152 us -> 0 us
  Pallas kernels: 0 us -> 147 us
  starting transfers between devices: 57.6 us -> 0 us
  local copies, waits for them, and re-layouts: 13.6 us -> 1.54 us
  other arithmetic: 6.47 us -> 0 us
  matrix products: 3.51 us -> 0 us
    all_to_all x3 -> x0, waiting for transfers between devices: 152 us -> none  [the longest x1 72.4 us: local(): lax.all_to_all(spinors, 'ta', split_axis=0, concat_axis=1, tiled=True)]
    pallas_call x0 -> x1, Pallas kernels: none -> 147 us  [local(): pl.pallas_call(functools.partial(kernel, sizes), out_shape=jax.ShapeDtype...]
    all_to_all x3 -> x0, starting transfers between devices: 57.6 us -> none  [the longest x1 43.9 us: local(): lax.all_to_all(spinors, 'ta', split_axis=0, concat_axis=1, tiled=True)]
    all_to_all x4 -> x0, local copies, waits for them, and re-layouts: 5.13 us -> none  [the longest x2 4.32 us: local(): lax.all_to_all(grouped, 'ta', split_axis=1, concat_axis=0, tiled=True)]
    dot_general x4 -> x0, matrix products: 3.51 us -> none  [contract(): jnp.einsum('tkcx,ntscx->tsnk', left_side, right_side, precision=lax.Preci...]
    slice x1 -> x0, local copies, waits for them, and re-layouts: 3.37 us -> none  [contract_pair(): vector_real = vectors[:, :, 0]]
    sort x2 -> x0, other arithmetic: 3.21 us -> none  [the longest x1 1.61 us: local(): inverse = jnp.argsort(source_ids)]
  transfers between devices with their start and end apart: 3 -> 0, of which waited for: 3 -> 0; matrix products, arithmetic and copies ran while one was open for 3% -> 0% of each run, Pallas kernels for 0% -> 0%
where the time goes in v1:
time: 148 us
  Pallas kernels  147 us (99%)
  local copies, waits for them, and re-layouts  1.54 us (1%)
    pallas_call x1, Pallas kernels, local(): pl.pallas_call(functools.partial(kernel, sizes), out_shape=jax.ShapeDtype...  147 us

profile of v1, /device:TPU:80, one launch (start us, length us, event | category | flops | bytes accessed | tf_op | source)
XLA Modules:
  0.0 148.1 jit_solution(5931237555474728934)
XLA Ops:
  0.0 146.6 %shard_map.46 = f32[2,2,16,128]{3,2,1,0:T(8,128)} custom-call(s32[32]{0:T(128)} %group_ref.1, s32[32]{0:T(128)} %ids_ref.1, f32[2,1536,128]{2,1,0:T(8,128)} %bitcast.19, f32[32,2,48,128]{3,2,1,0:T(8,128)} %bitcast.20), custom_call_target="tpu_custom_call" | custom-call | tf_op jit(solution)/shard_map/pallas_call | solution.py:285
  146.6 0.9 reshape.19
  147.4 0.7 copy.9

commit v2 on v1

--- a/solution.py
+++ b/solution.py
@@ -14,7 +14,7 @@
 
 def kernel(sizes, group_ref, ids_ref, vec_ref, spin_ref, out_ref,
            rank, order, inverse, raw, both, high, low, mids, mail, gathered, left,
-           part, parts, home, relay, post, back,
+           part, parts, home, relay, post, back, flat,
            load_sem, own_sem, pair_sem, s1, r1, s2, r2, s3, r3, s4, r4, s5, r5):
     nz, nx, nc, ns, nt, spin, depth, keep = sizes
     z, x, c = lax.axis_index("ta"), lax.axis_index("xyz"), lax.axis_index("src")
@@ -58,9 +58,9 @@
             src_ref=mail.at[q, d], dst_ref=gathered.at[q, :, pl.ds(pl.multiple_of(z * chunk, 8), chunk), :],
             send_sem=s2.at[q, d], recv_sem=r2.at[q, d], device_id={"ta": far(d)}, device_id_type=MESH)
 
-    for q in range(Q):
-        @pl.loop(1, nz)
-        def _(d):
+    outward = sorted(range(1, nz), key=lambda d: -min(d, nz - d))
+    for q in range(Q):
+        for d in outward:
             spread(q, d).start()
 
         pltpu.make_async_copy(share(q, z), mids[q].at[pl.ds(nt * z, nt)], own_sem.at[q]).start()
@@ -115,9 +115,10 @@
                 low[tl, core * rows:(core + 1) * rows, g * LANES:(g + 1) * LANES] = (block - top.astype(jnp.float32)).astype(jnp.bfloat16)
 
     for q in range(Q):
-        @pl.loop(1, nz)
-        def _(d):
-            spread(q, d).wait_recv()
+        with jax.named_scope("mid%d" % q):
+            @pl.loop(1, nz)
+            def _(d):
+                spread(q, d).wait_recv()
 
         pltpu.make_async_copy(share(q, z), mids[q].at[pl.ds(nt * z, nt)], own_sem.at[q]).wait()
 
@@ -129,8 +130,7 @@
         for tl in range(nt):
             gathered[q, tl, pl.ds(pl.multiple_of(z * chunk, 8), chunk), :] = mids[q][rank[nt * z + tl]]
 
-        @pl.loop(1, nz)
-        def _(d):
+        for d in outward:
             deliver(q, d).start()
 
     contract = (((1,), (1,)), ((), ()))
@@ -144,10 +144,20 @@
             device_id={"xyz": half * c + xs, "src": core}, device_id_type=MESH)
 
     sender = lax.div(x, half)
-    for q in range(Q):
-        @pl.loop(1, nz)
-        def _(d):
-            deliver(q, d).wait_recv()
+    per = nz // (Q * 2)
+    relays = 2 * per
+    step = ks // half
+
+    def relay_at(i):
+        return lax.rem(i + nz - relays // 4, nz)
+
+    my_relay = lax.rem(z + relays // 4, nz)
+
+    def contract_chunk(q):
+        with jax.named_scope("got%d" % q):
+            @pl.loop(1, nz)
+            def _(d):
+                deliver(q, d).wait_recv()
 
         for tl in range(nt):
             for i in range(colours):
@@ -167,7 +177,6 @@
             one = lax.dot_general(left[...], high[tl], contract, preferred_element_type=jnp.float32)
             two = lax.dot_general(left[0:2 * ks, :], low[tl], contract, preferred_element_type=jnp.float32)
             total = one[0:2 * ks] + one[2 * ks:4 * ks] + two
-            step = ks // half
             for xs in range(half):
                 for core in range(nc):
                     for reim in range(2):
@@ -185,24 +194,34 @@
                 def _():
                     parts[q, x] = part[q, xs, core]
 
-    def return_copy(d):
-        return pltpu.make_async_remote_copy(
-            src_ref=home.at[far(d)], dst_ref=relay.at[pl.ds(nt * z, nt)],
-            send_sem=s4.at[d], recv_sem=r4.at[d], device_id={"ta": far(d)}, device_id_type=MESH)
-
-    def final_copy(d):
-        return pltpu.make_async_remote_copy(
-            src_ref=post.at[far(d)], dst_ref=back.at[z],
-            send_sem=s5.at[d], recv_sem=r5.at[d], device_id={"ta": far(d)}, device_id_type=MESH)
-
-    per = nz // (Q * 2)
-    for q in range(Q):
-        for xs in range(nx):
-            @pl.when(jnp.logical_not(jnp.logical_and(xs == x, sender == c)))
-            def _():
-                pltpu.make_async_remote_copy(
-                    src_ref=part.at[q, 0, 0], dst_ref=parts.at[q, xs], send_sem=s3.at[q, 0, 0], recv_sem=r3.at[q, xs],
-                    device_id={"src": other}, device_id_type=MESH).wait_recv()
+    def return_copy(q, i):
+        return pltpu.make_async_remote_copy(
+            src_ref=home.at[q, i], dst_ref=relay[q].at[pl.ds(nt * z, nt)],
+            send_sem=s4.at[q, i], recv_sem=r4.at[q, z], device_id={"ta": relay_at(i)}, device_id_type=MESH)
+
+    def arrival(q, there):
+        return pltpu.make_async_remote_copy(
+            src_ref=home.at[q, 0], dst_ref=relay[q].at[pl.ds(nt * there, nt)],
+            send_sem=s4.at[q, 0], recv_sem=r4.at[q, there], device_id={"src": other}, device_id_type=MESH)
+
+    def final_copy(q, d):
+        return pltpu.make_async_remote_copy(
+            src_ref=post.at[q, far(d)], dst_ref=back.at[q, my_relay],
+            send_sem=s5.at[q, d], recv_sem=r5.at[q, my_relay], device_id={"ta": far(d)}, device_id_type=MESH)
+
+    def final_arrival(q, i):
+        return pltpu.make_async_remote_copy(
+            src_ref=post.at[q, 0], dst_ref=back.at[q, i],
+            send_sem=s5.at[q, 0], recv_sem=r5.at[q, i], device_id={"src": other}, device_id_type=MESH)
+
+    def reduce_chunk(q):
+        with jax.named_scope("reduced%d" % q):
+            for xs in range(nx):
+                @pl.when(jnp.logical_not(jnp.logical_and(xs == x, sender == c)))
+                def _():
+                    pltpu.make_async_remote_copy(
+                        src_ref=part.at[q, 0, 0], dst_ref=parts.at[q, xs], send_sem=s3.at[q, 0, 0], recv_sem=r3.at[q, xs],
+                        device_id={"src": other}, device_id_type=MESH).wait_recv()
 
         for tl in range(nt):
             for reim in range(2):
@@ -210,57 +229,86 @@
                 for xs in range(1, nx):
                     total += parts[q, xs, tl, reim]
                 for i in range(per):
-                    home[(q * 2 + reim) * per + i, tl] = total[i * keep:(i + 1) * keep, :]
-
-    @pl.loop(1, nz)
-    def _(d):
-        return_copy(d).start()
-
-    for tl in range(nt):
-        relay[nt * z + tl] = home[z, tl]
-
-    @pl.loop(1, nz)
-    def _(d):
-        return_copy(d).wait_recv()
-
-    @pl.loop(0, nz)
-    def _(there):
-        for tl in range(nt):
-            post[there, tl] = relay[order[nt * there + tl]]
-
-    @pl.loop(1, nz)
-    def _(d):
-        final_copy(d).start()
-
-    back[z] = post[z]
-
-    @pl.loop(1, nz)
-    def _(d):
-        final_copy(d).wait_recv()
-
-    for q in range(Q):
+                    home[q, reim * per + i, tl] = total[i * keep:(i + 1) * keep, :]
+
+        for i in range(relays):
+            @pl.when(relay_at(i) != z)
+            def _():
+                return_copy(q, i).start()
+
+            @pl.when(relay_at(i) == z)
+            def _():
+                for tl in range(nt):
+                    relay[q][nt * z + tl] = home[q, i, tl]
+
+    def relay_chunk(q):
+        @pl.when(my_relay < relays)
+        def _():
+            with jax.named_scope("relayed%d" % q):
+                @pl.loop(0, nz)
+                def _(there):
+                    @pl.when(there != z)
+                    def _():
+                        arrival(q, there).wait_recv()
+
+            @pl.loop(0, nz)
+            def _(there):
+                for tl in range(nt):
+                    post[q, there, tl] = relay[q][order[nt * there + tl]]
+
+            for d in range(1, nz):
+                final_copy(q, d).start()
+
+            back[q, my_relay] = post[q, z]
+
+    contract_chunk(0)
+    for q in range(Q):
+        reduce_chunk(q)
+        if q + 1 < Q:
+            contract_chunk(q + 1)
+            relay_chunk(q)
+    relay_chunk(Q - 1)
+
+    for q in range(Q):
+        @pl.loop(1, nz)
+        def _(d):
+            spread(q, d).wait_send()
+            deliver(q, d).wait_send()
+
+        for xs in range(half):
+            for core in range(nc):
+                @pl.when(jnp.logical_not(jnp.logical_and(half * c + xs == x, c == core)))
+                def _():
+                    reduce_copy(q, xs, core).wait_send()
+
+        for i in range(relays):
+            @pl.when(relay_at(i) != z)
+            def _():
+                return_copy(q, i).wait_send()
+
+    for q in range(Q):
+        with jax.named_scope("final%d" % q):
+            @pl.loop(0, relays)
+            def _(i):
+                @pl.when(i != my_relay)
+                def _():
+                    final_arrival(q, i).wait_recv()
+
         for reim in range(2):
             for i in range(per):
                 for tl in range(nt):
                     at = i * Q * keep + q * keep
-                    out_ref[tl, reim, at:at + keep, :] = back[(q * 2 + reim) * per + i, tl]
-
-    for q in range(Q):
-        @pl.loop(1, nz)
-        def _(d):
-            spread(q, d).wait_send()
-            deliver(q, d).wait_send()
-
-        for xs in range(half):
-            for core in range(nc):
-                @pl.when(jnp.logical_not(jnp.logical_and(half * c + xs == x, c == core)))
-                def _():
-                    reduce_copy(q, xs, core).wait_send()
-
-    @pl.loop(1, nz)
-    def _(d):
-        return_copy(d).wait_send()
-        final_copy(d).wait_send()
+                    flat[tl, reim, at:at + keep, :] = back[q, reim * per + i, tl]
+
+    for s in range(spin):
+        out_ref[:, :, s] = flat[:, :, :, s * ns:(s + 1) * ns]
+
+    @pl.when(my_relay < relays)
+    def _():
+        for q in range(Q):
+            @pl.loop(1, nz)
+            def _(d):
+                final_copy(q, d).wait_send()
 
 
 def solution(mesh):
@@ -282,9 +330,9 @@
         f32, bf16 = jnp.float32, jnp.bfloat16
         dma = pltpu.SemaphoreType.DMA
         small = (keep, LANES)
-        flat = pl.pallas_call(
+        out = pl.pallas_call(
             functools.partial(kernel, sizes),
-            out_shape=jax.ShapeDtypeStruct((nt, 2, kk // nx, rows), f32),
+            out_shape=jax.ShapeDtypeStruct((nt, 2, spin, kk // nx, ns), f32),
             in_specs=[pl.BlockSpec(memory_space=pltpu.SMEM)] * 2 + [pl.BlockSpec(memory_space=pl.ANY)] * 2,
             out_specs=pl.BlockSpec(memory_space=pltpu.VMEM),
             scratch_shapes=[
@@ -301,18 +349,19 @@
                 pltpu.VMEM((4 * ks, depth * LANES), bf16),
                 pltpu.VMEM((Q, nx // nc, nc, nt, 2, ks * nc // nx, LANES), f32),
                 pltpu.VMEM((Q, nx, nt, 2, ks * nc // nx, LANES), f32),
-                pltpu.VMEM((nz, nt) + small, f32),
-                pltpu.VMEM((nz * nt,) + small, f32),
-                pltpu.VMEM((nz, nt) + small, f32),
-                pltpu.VMEM((nz, nt) + small, f32),
+                pltpu.VMEM((Q, nz // Q, nt) + small, f32),
+                [pltpu.VMEM((nz * nt,) + small, f32)] * Q,
+                pltpu.VMEM((Q, nz, nt) + small, f32),
+                pltpu.VMEM((Q, nz // Q, nt) + small, f32),
+                pltpu.VMEM((nt, 2, kk // nx, rows), f32),
                 dma, dma((Q,)), dma((2,)),
                 dma((Q, nz)), dma((Q, nz)), dma((Q, nz)), dma((Q, nz)),
                 dma((Q, nx // nc, nc)), dma((Q, nx)),
-                dma((nz,)), dma((nz,)), dma((nz,)), dma((nz,)),
+                dma((Q, nz // Q)), dma((Q, nz)), dma((Q, nz)), dma((Q, nz // Q)),
             ],
             compiler_params=pltpu.CompilerParams(collective_id=0, has_side_effects=True),
         )(group_of, source_ids, vec_view, spin_view)
-        return flat.reshape(nt, 2, kk // nx, spin, ns).transpose(0, 1, 3, 4, 2)
+        return out.transpose(0, 1, 2, 4, 3)
 
     in_specs = (
         P("src", "ta", None, "job", None, "xyz"),

time: 148 us -> 143 us (0.966)
  Pallas kernels: 147 us -> 141 us
    pallas_call x1, Pallas kernels: 147 us -> 141 us  [local(): pl.pallas_call(functools.partial(kernel, sizes), out_shape=jax.ShapeDtype...]
    unnamed x0 -> x1, local copies, waits for them, and re-layouts: none -> 1.57 us
    reshape x2 -> x0, local copies, waits for them, and re-layouts: 1.54 us -> none  [local(): return flat.reshape(nt, 2, kk // nx, spin, ns).transpose(0, 1, 3, 4, 2)]
where the time goes in v2:
time: 143 us
  Pallas kernels  141 us (99%)
  local copies, waits for them, and re-layouts  1.57 us (1%)
    pallas_call x1, Pallas kernels, local(): pl.pallas_call(functools.partial(kernel, sizes), out_shape=jax.ShapeDtype...  141 us

profile of v2, /device:TPU:80, one launch (start us, length us, event | category | flops | bytes accessed | tf_op | source)
XLA Modules:
  0.0 142.6 jit_solution(4182652454443000955)
XLA Ops:
  0.0 141.0 %shard_map.46 = f32[2,2,4,16,32]{4,3,2,1,0:T(8,128)} custom-call(s32[32]{0:T(128)} %group_ref.1, s32[32]{0:T(128)} %ids_ref.1, f32[2,1536,128]{2,1,0:T(8,128)} %bitcast.15, f32[32,2,48,128]{3,2,1,0:T(8,128)} %bitcast.16), custom_call_target="tpu_custom_call" | custom-call | tf_op jit(solution)/shard_map/pallas_call | solution.py:333
  141.0 1.6 %copy.8 = f32[2,2,4,32,16]{3,4,2,1,0:T(8,128)} copy(f32[2,2,4,32,16]{3,4,2,1,0:T(8,128)} %bitcast.17) | data formatting | bytes 65536

commit v3 on v2

v3 whole, which is shorter than its diff:
```python
import functools

import jax
import jax.numpy as jnp
from jax import lax
from jax.experimental import pallas as pl
from jax.experimental.pallas import tpu as pltpu
from jax.sharding import PartitionSpec as P

MESH = pl.DeviceIdType.MESH
LANES = 128
Q = 2
EARLY = 12
LATE = 0
RELAYS = 4
BEFORE = 1


def kernel(sizes, group_hbm, ids_hbm, vec_ref, spin_ref, out_ref,
           group_ref, ids_ref, rank, order, inverse, raw, both, high, low, mids, mail, gathered, left,
           part, parts, home, relay, post, back, flat,
           above, along, small_sem, load_sem, own_sem, pair_sem, *pairs):
    (s1, r1), (s2, r2), (s3, r3), (s4, r4), (s5, r5) = pairs
    nz, nx, nc, ns, nt, spin, depth, keep, relays = sizes
    z, x, c = lax.axis_index("ta"), lax.axis_index("xyz"), lax.axis_index("src")
    other = 1 - c
    rows = ns * spin
    chunk = keep * depth
    half = nx // nc

    def far(d):
        return lax.rem(z + d, nz)

    def settle(ref, sem):
        pltpu.make_async_copy(ref, ref, sem).wait()

    place = lax.rem(z + nz - 1, nz)

    def at_place(p):
        return lax.rem(p + 1, nz)

    barrier = pltpu.get_barrier_semaphore()

    @pl.loop(0, nz - 1 - place)
    def _(i):
        pl.semaphore_signal(barrier, inc=1, device_id={"ta": at_place(nz - 1 - i)}, device_id_type=MESH)

    right, left_x = lax.rem(x + 1, nx), lax.rem(x + nx - 1, nx)
    for there in (right, left_x):
        pl.semaphore_signal(barrier, inc=1, device_id={"xyz": there}, device_id_type=MESH)
    pl.semaphore_signal(barrier, inc=1, device_id={"src": other}, device_id_type=MESH)

    loads = [
        pltpu.make_async_copy(group_hbm, group_ref, small_sem.at[0]),
        pltpu.make_async_copy(ids_hbm, ids_ref, small_sem.at[1]),
        pltpu.make_async_copy(spin_ref, raw, load_sem),
    ]
    for load in loads:
        load.start()
    pl.semaphore_wait(barrier, 3 + place)

    def share(q, there):
        first = (c * (nz * Q * keep) + there * (Q * keep) + q * keep) * depth
        return vec_ref.at[:, pl.ds(pl.multiple_of(first, 8), chunk), :]

    def spread(q, d):
        return pltpu.make_async_remote_copy(
            src_ref=share(q, far(d)), dst_ref=mids[q].at[pl.ds(nt * z, nt)],
            send_sem=s1.at[q], recv_sem=r1.at[q], device_id={"ta": far(d)}, device_id_type=MESH)

    def deliver(q, d):
        return pltpu.make_async_remote_copy(
            src_ref=mail.at[q, d], dst_ref=gathered.at[q, :, pl.ds(pl.multiple_of(z * chunk, 8), chunk), :],
            send_sem=s2.at[q], recv_sem=r2.at[q], device_id={"ta": far(d)}, device_id_type=MESH)

    outward = sorted(range(1, nz), key=lambda d: -min(d, nz - d))
    with jax.named_scope("known"):
      for d in outward:
        @pl.when(d >= nz - place)
        def _():
            pl.semaphore_signal(above.at[place], inc=1, device_id={"ta": far(d)}, device_id_type=MESH)

    for q in range(Q):
        for d in outward:
            @pl.when(d >= nz - place)
            def _():
                spread(q, d).start()

        pltpu.make_async_copy(share(q, z), mids[q].at[pl.ds(nt * z, nt)], own_sem.at[q]).start()

    count = nz * nt

    def prepare():
        hops = list(range(nx // 2 - 1))

        def tell(j):
            pl.semaphore_signal(along.at[0, j], inc=1, device_id={"xyz": left_x}, device_id_type=MESH)
            pl.semaphore_signal(along.at[1, j], inc=1, device_id={"xyz": right}, device_id_type=MESH)

        def hear(j):
            pl.semaphore_wait(along.at[0, j], 1)
            pl.semaphore_wait(along.at[1, j], 1)

        tell(hops[0])
        loads[0].wait()
        loads[1].wait()


        @pl.loop(0, count)
        def _(t):
            mine = group_ref[t] * count + t
            total = jnp.int32(0)
            for u in range(count):
                total += jnp.where(group_ref[u] * count + u < mine, 1, 0)
            rank[t] = total

        @pl.loop(0, count)
        def _(r):
            total = jnp.int32(0)
            for u in range(count):
                total = jnp.maximum(total, jnp.where(rank[u] == r, u, 0))
            order[r] = total

        @pl.loop(0, ns)
        def _(j):
            total = jnp.int32(0)
            for u in range(ns):
                total = jnp.maximum(total, jnp.where(ids_ref[u] - c * ns == j, u, 0))
            inverse[j] = total

        for j in hops[:-1]:
            hear(j)
            tell(j + 1)
        loads[2].wait()

        @pl.loop(0, ns)
        def _(j):
            n = inverse[j]
            for tl in range(nt):
                for g in range(depth):
                    for s in range(spin):
                        both[c, tl, g, pl.ds(s * ns + j, 1), :] = raw[n, tl, g * spin + s:g * spin + s + 1, :]

        pair = pltpu.make_async_remote_copy(
            src_ref=both.at[c], dst_ref=both.at[c], send_sem=pair_sem.at[0], recv_sem=pair_sem.at[1],
            device_id={"src": other}, device_id_type=MESH)
        hear(hops[-1])
        pair.start()
        pair.wait()

        @pl.loop(0, nt)
        def _(tl):
            for core in range(nc):
                for g in range(depth):
                    block = both[core, tl, g]
                    top = block.astype(jnp.bfloat16)
                    high[tl, core * rows:(core + 1) * rows, g * LANES:(g + 1) * LANES] = top
                    low[tl, core * rows:(core + 1) * rows, g * LANES:(g + 1) * LANES] = (block - top.astype(jnp.float32)).astype(jnp.bfloat16)

    with jax.named_scope("early"):
        @pl.when(place < EARLY)
        def _():
            prepare()

    with jax.named_scope("upper"):
        @pl.loop(1, jnp.maximum(LATE - place, 1))
        def _(d):
            pl.semaphore_wait(above.at[place + d], 1)
            for q in range(Q):
                spread(q, d).start()

        @pl.loop(jnp.maximum(LATE - place, 1), nz - place)
        def _(d):
            pl.semaphore_wait(above.at[place + d], 1)
            spread(0, d).start()

        for q in range(1, Q):
            for d in outward:
                @pl.when(jnp.logical_and(place + d >= LATE, place + d < nz))
                def _():
                    spread(q, d).start()

    with jax.named_scope("late"):
        @pl.when(place >= EARLY)
        def _():
            prepare()

    for q in range(Q):
        with jax.named_scope("mid%d" % q):
            settle(mids[q].at[pl.ds(0, nt * (nz - 1))], r1.at[q])

        pltpu.make_async_copy(share(q, z), mids[q].at[pl.ds(nt * z, nt)], own_sem.at[q]).wait()

        @pl.loop(1, nz)
        def _(d):
            for tl in range(nt):
                mail[q, d, tl] = mids[q][rank[nt * far(d) + tl]]

        for tl in range(nt):
            gathered[q, tl, pl.ds(pl.multiple_of(z * chunk, 8), chunk), :] = mids[q][rank[nt * z + tl]]

        for d in outward:
            deliver(q, d).start()

    contract = (((1,), (1,)), ((), ()))
    ks = nz * keep
    colours = depth // 4

    def target(o):
        return lax.rem(x + o, half)

    def reduce_copy(q, o, core):
        xs = target(o)
        return pltpu.make_async_remote_copy(
            src_ref=part.at[q, xs * nc + core], dst_ref=parts.at[q, x],
            send_sem=s3.at[q], recv_sem=r3.at[q],
            device_id={"xyz": half * c + xs, "src": core}, device_id_type=MESH)

    sender = lax.div(x, half)
    step = ks // half
    per = relays // 2
    piece = step // per

    def relay_at(i):
        return lax.rem(i + nz - BEFORE, nz)

    my_relay = lax.rem(z + BEFORE, nz)

    def contract_chunk(q):
        with jax.named_scope("got%d" % q):
            settle(gathered.at[q, :, pl.ds(0, (nz - 1) * chunk)], r2.at[q])

        for tl in range(nt):
            for i in range(colours):
                for b in range(2):
                    re = gathered[q, tl, pl.ds(i * 4 + b * 2, ks, stride=depth), :]
                    im = gathered[q, tl, pl.ds(i * 4 + b * 2 + 1, ks, stride=depth), :]
                    g = i * 2 + b
                    for at, value in ((0, re), (depth // 2, im)):
                        top = value.astype(jnp.bfloat16)
                        rest = (value - top.astype(jnp.float32)).astype(jnp.bfloat16)
                        where = slice((at + g) * LANES, (at + g + 1) * LANES)
                        cross = slice((depth // 2 - at + g) * LANES, (depth // 2 - at + g + 1) * LANES)
                        left[0:ks, where] = top
                        left[2 * ks:3 * ks, where] = rest
                        left[ks:2 * ks, cross] = top if at == 0 else -top
                        left[3 * ks:4 * ks, cross] = rest if at == 0 else -rest
            one = lax.dot_general(left[...], high[tl], contract, preferred_element_type=jnp.float32)
            two = lax.dot_general(left[0:2 * ks, :], low[tl], contract, preferred_element_type=jnp.float32)
            total = one[0:2 * ks] + one[2 * ks:4 * ks] + two
            for xs in range(half):
                for core in range(nc):
                    for reim in range(2):
                        part[q, xs * nc + core, tl, reim] = total[reim * ks + xs * step:reim * ks + (xs + 1) * step, core * rows:(core + 1) * rows]

        for o in [0] + sorted(range(1, half), key=lambda o: abs(2 * o - half)):
            for core in range(nc):
                mine = jnp.logical_and(half * c + target(o) == x, c == core)

                @pl.when(jnp.logical_not(mine))
                def _():
                    reduce_copy(q, o, core).start()

                if o == 0:
                    @pl.when(mine)
                    def _():
                        parts[q, x] = part[q, target(o) * nc + core]

    def return_copy(q, i):
        return pltpu.make_async_remote_copy(
            src_ref=home.at[q, i], dst_ref=relay[q].at[pl.ds(nt * z, nt)],
            send_sem=s4.at[q], recv_sem=r4.at[q], device_id={"ta": relay_at(i)}, device_id_type=MESH)

    def final_copy(q, there):
        return pltpu.make_async_remote_copy(
            src_ref=post.at[q, there], dst_ref=back.at[q, my_relay],
            send_sem=s5.at[q], recv_sem=r5.at[q], device_id={"ta": there}, device_id_type=MESH)

    def reduce_chunk(q):
        with jax.named_scope("reduced%d" % q):
            @pl.when(sender == c)
            def _():
                settle(parts.at[q, pl.ds(0, nx - 1)], r3.at[q])

            @pl.when(sender != c)
            def _():
                settle(parts.at[q], r3.at[q])

        for tl in range(nt):
            for reim in range(2):
                total = parts[q, 0, tl, reim]
                for xs in range(1, nx):
                    total += parts[q, xs, tl, reim]
                for i in range(per):
                    home[q, reim * per + i, tl] = total[i * piece:(i + 1) * piece, :]

        for i in range(relays):
            @pl.when(relay_at(i) != z)
            def _():
                return_copy(q, i).start()

            @pl.when(relay_at(i) == z)
            def _():
                for tl in range(nt):
                    relay[q][nt * z + tl] = home[q, i, tl]

    def relay_chunk(q):
        @pl.when(my_relay < relays)
        def _():
            with jax.named_scope("relayed%d" % q):
                settle(relay[q].at[pl.ds(0, nt * (nz - 1))], r4.at[q])

            for there in range(nz):
                for tl in range(nt):
                    post[q, there, tl] = relay[q][order[nt * there + tl]]

                @pl.when(there != z)
                def _():
                    final_copy(q, there).start()

            back[q, my_relay] = post[q, z]

    for q in range(Q):
        contract_chunk(q)
        reduce_chunk(q)
    for q in range(Q):
        relay_chunk(q)

    for q in range(Q):
        settle(mids[q].at[pl.ds(0, nt * (nz - 1))], s1.at[q])
        settle(mail.at[q, pl.ds(0, nz - 1)], s2.at[q])

        @pl.when(sender == c)
        def _():
            settle(part.at[q, pl.ds(0, nx - 1)], s3.at[q])

        @pl.when(sender != c)
        def _():
            settle(part.at[q], s3.at[q])

        @pl.when(my_relay < relays)
        def _():
            settle(home.at[q, pl.ds(0, relays - 1)], s4.at[q])
            settle(post.at[q, pl.ds(0, nz - 1)], s5.at[q])

        @pl.when(my_relay >= relays)
        def _():
            settle(home.at[q], s4.at[q])

    for q in range(Q):
        with jax.named_scope("final%d" % q):
            @pl.when(my_relay < relays)
            def _():
                settle(back.at[q, pl.ds(0, relays - 1)], r5.at[q])

            @pl.when(my_relay >= relays)
            def _():
                settle(back.at[q], r5.at[q])

        with jax.named_scope("asm%d" % q):
            for reim in range(2):
                for i in range(per):
                    for tl in range(nt):
                        got = back[q, reim * per + i, tl]
                        for j in range(piece // keep):
                            at = (i * (piece // keep) + j) * Q * keep + q * keep
                            flat[tl, reim, at:at + keep, :] = got[j * keep:(j + 1) * keep, :]

    with jax.named_scope("outs"):
        for s in range(spin):
            out_ref[:, :, s] = flat[:, :, :, s * ns:(s + 1) * ns]


def solution(mesh):
    nz, nx, nc = mesh.shape["ta"], mesh.shape["xyz"], mesh.shape["src"]

    def local(spinors, eigvecs, group_of, source_ids):
        ns, nt, _, spin, colours, sites = spinors.shape
        kk = eigvecs.shape[1]
        blocks = sites // LANES
        depth = 2 * colours * blocks
        keep = kk // (nc * nz * Q)
        rows = ns * spin
        ks = nz * keep
        spin_view = spinors.transpose(0, 1, 2, 4, 3, 5).reshape(ns, nt, 2, colours, spin, blocks, LANES)
        spin_view = spin_view.transpose(0, 1, 2, 3, 5, 4, 6).reshape(ns, nt, depth * spin, LANES)
        vec_view = eigvecs.transpose(0, 1, 3, 2, 4).reshape(nt, kk, colours, 2, blocks, LANES)
        vec_view = vec_view.transpose(0, 1, 2, 4, 3, 5).reshape(nt, kk * depth, LANES)
        step = ks * nc // nx
        relays = RELAYS
        sizes = (nz, nx, nc, ns, nt, spin, depth, keep, relays)
        f32, bf16 = jnp.float32, jnp.bfloat16
        dma = pltpu.SemaphoreType.DMA
        small = (step * 2 // relays, LANES)
        out = pl.pallas_call(
            functools.partial(kernel, sizes),
            out_shape=jax.ShapeDtypeStruct((nt, 2, spin, kk // nx, ns), f32),
            in_specs=[pl.BlockSpec(memory_space=pl.ANY)] * 4,
            out_specs=pl.BlockSpec(memory_space=pltpu.VMEM),
            scratch_shapes=[
                pltpu.SMEM((nz * nt,), jnp.int32),
                pltpu.SMEM((ns,), jnp.int32),
                pltpu.SMEM((nz * nt,), jnp.int32),
                pltpu.SMEM((nz * nt,), jnp.int32),
                pltpu.SMEM((ns,), jnp.int32),
                pltpu.VMEM((ns, nt, depth * spin, LANES), f32),
                pltpu.VMEM((nc, nt, depth, rows, LANES), f32),
                pltpu.VMEM((nt, nc * rows, depth * LANES), bf16),
                pltpu.VMEM((nt, nc * rows, depth * LANES), bf16),
                [pltpu.VMEM((nz * nt, keep * depth, LANES), f32)] * Q,
                pltpu.VMEM((Q, nz, nt, keep * depth, LANES), f32),
                pltpu.VMEM((Q, nt, ks * depth, LANES), f32),
                pltpu.VMEM((4 * ks, depth * LANES), bf16),
                pltpu.VMEM((Q, nx, nt, 2, ks * nc // nx, LANES), f32),
                pltpu.VMEM((Q, nx, nt, 2, ks * nc // nx, LANES), f32),
                pltpu.VMEM((Q, relays, nt) + small, f32),
                [pltpu.VMEM((nz * nt,) + small, f32)] * Q,
                pltpu.VMEM((Q, nz, nt) + small, f32),
                pltpu.VMEM((Q, relays, nt) + small, f32),
                pltpu.VMEM((nt, 2, kk // nx, rows), f32),
                pltpu.SemaphoreType.REGULAR((nz,)), pltpu.SemaphoreType.REGULAR((2, nx // 2 - 1)), dma((2,)), dma, dma((Q,)), dma((2,)),
                [dma((Q,))] * 2, [dma((Q,))] * 2, [dma((Q,))] * 2, [dma((Q,))] * 2, [dma((Q,))] * 2,
            ],
            compiler_params=pltpu.CompilerParams(collective_id=0, has_side_effects=True),
        )(group_of, source_ids, vec_view, spin_view)
        return out.transpose(0, 1, 2, 4, 3)

    in_specs = (
        P("src", "ta", None, "job", None, "xyz"),
        P("ta", "job", None, None, "xyz"),
        P(),
        P("src"),
    )
    out_specs = P("ta", None, "job", "src", "xyz")
    return jax.shard_map(local, mesh=mesh, in_specs=in_specs, out_specs=out_specs, check_vma=False)
```

time: 143 us -> 134 us (0.937)
  Pallas kernels: 141 us -> 132 us
    pallas_call x1, Pallas kernels: 141 us -> 132 us  [local(): pl.pallas_call(functools.partial(kernel, sizes), out_shape=jax.ShapeDtype...]
where the time goes in v3:
time: 134 us
  Pallas kernels  132 us (99%)
  local copies, waits for them, and re-layouts  1.57 us (1%)
    pallas_call x1, Pallas kernels, local(): pl.pallas_call(functools.partial(kernel, sizes), out_shape=jax.ShapeDtype...  132 us

profile of v3, /device:TPU:80, one launch (start us, length us, event | category | flops | bytes accessed | tf_op | source)
XLA Modules:
  0.0 134.0 jit_solution(18143738483031701511)
XLA Ops:
  0.0 132.4 %shard_map.46 = f32[2,2,4,16,32]{4,3,2,1,0:T(8,128)} custom-call(s32[32]{0:T(128)} %group_hbm.1, s32[32]{0:T(128)} %ids_hbm.1, f32[2,1536,128]{2,1,0:T(8,128)} %bitcast.15, f32[32,2,48,128]{3,2,1,0:T(8,128)} %bitcast.16), custom_call_target="tpu_custom_call" | custom-call | tf_op jit(solution)/shard_map/pallas_call | solution.py:395
  132.4 1.6 %copy.8 = f32[2,2,4,32,16]{3,4,2,1,0:T(8,128)} copy(f32[2,2,4,32,16]{3,4,2,1,0:T(8,128)} %bitcast.17) | data formatting | bytes 65536

commit v4 on v3

--- a/solution.py
+++ b/solution.py
@@ -13,7 +13,7 @@
 EARLY = 12
 LATE = 0
 RELAYS = 4
-BEFORE = 1
+BEFORE = 3
 
 
 def kernel(sizes, group_hbm, ids_hbm, vec_ref, spin_ref, out_ref,
@@ -209,10 +209,10 @@
     def target(o):
         return lax.rem(x + o, half)
 
-    def reduce_copy(q, o, core):
+    def reduce_copy(q, o, core, tl):
         xs = target(o)
         return pltpu.make_async_remote_copy(
-            src_ref=part.at[q, xs * nc + core], dst_ref=parts.at[q, x],
+            src_ref=part.at[q, xs * nc + core, tl], dst_ref=parts.at[q, x, tl],
             send_sem=s3.at[q], recv_sem=r3.at[q],
             device_id={"xyz": half * c + xs, "src": core}, device_id_type=MESH)
 
@@ -253,18 +253,18 @@
                     for reim in range(2):
                         part[q, xs * nc + core, tl, reim] = total[reim * ks + xs * step:reim * ks + (xs + 1) * step, core * rows:(core + 1) * rows]
 
-        for o in [0] + sorted(range(1, half), key=lambda o: abs(2 * o - half)):
-            for core in range(nc):
-                mine = jnp.logical_and(half * c + target(o) == x, c == core)
-
-                @pl.when(jnp.logical_not(mine))
-                def _():
-                    reduce_copy(q, o, core).start()
-
-                if o == 0:
-                    @pl.when(mine)
+            for o in [0] + sorted(range(1, half), key=lambda o: abs(2 * o - half)):
+                for core in range(nc):
+                    mine = jnp.logical_and(half * c + target(o) == x, c == core)
+
+                    @pl.when(jnp.logical_not(mine))
                     def _():
-                        parts[q, x] = part[q, target(o) * nc + core]
+                        reduce_copy(q, o, core, tl).start()
+
+                    if o == 0:
+                        @pl.when(mine)
+                        def _():
+                            parts[q, x, tl] = part[q, target(o) * nc + core, tl]
 
     def return_copy(q, i):
         return pltpu.make_async_remote_copy(
@@ -322,6 +322,7 @@
 
     for q in range(Q):
         contract_chunk(q)
+    for q in range(Q):
         reduce_chunk(q)
     for q in range(Q):
         relay_chunk(q)

time: 134 us -> 133 us (level)
  no operation moved by 1% of the time
where the time goes in v4:
time: 133 us
  Pallas kernels  131 us (98%)
  local copies, waits for them, and re-layouts  1.57 us (1%)
    pallas_call x1, Pallas kernels, local(): pl.pallas_call(functools.partial(kernel, sizes), out_shape=jax.ShapeDtype...  131 us

profile of v4, /device:TPU:80, one launch (start us, length us, event | category | flops | bytes accessed | tf_op | source)
XLA Modules:
  0.0 133.1 jit_solution(14906109865732242851)
XLA Ops:
  0.0 131.5 %shard_map.46 = f32[2,2,4,16,32]{4,3,2,1,0:T(8,128)} custom-call(s32[32]{0:T(128)} %group_hbm.1, s32[32]{0:T(128)} %ids_hbm.1, f32[2,1536,128]{2,1,0:T(8,128)} %bitcast.15, f32[32,2,48,128]{3,2,1,0:T(8,128)} %bitcast.16), custom_call_target="tpu_custom_call" | custom-call | tf_op jit(solution)/shard_map/pallas_call | solution.py:396
  131.5 1.6 %copy.8 = f32[2,2,4,32,16]{3,4,2,1,0:T(8,128)} copy(f32[2,2,4,32,16]{3,4,2,1,0:T(8,128)} %bitcast.17) | data formatting | bytes 65536

commit v5 on v4

--- a/solution.py
+++ b/solution.py
@@ -10,7 +10,7 @@
 MESH = pl.DeviceIdType.MESH
 LANES = 128
 Q = 2
-EARLY = 12
+EARLY = 9
 LATE = 0
 RELAYS = 4
 BEFORE = 3

time: 133 us -> 132 us (level)
  no operation moved by 1% of the time
where the time goes in v5:
time: 132 us
  Pallas kernels  130 us (98%)
  local copies, waits for them, and re-layouts  1.57 us (1%)
    pallas_call x1, Pallas kernels, local(): pl.pallas_call(functools.partial(kernel, sizes), out_shape=jax.ShapeDtype...  130 us

profile of v5, /device:TPU:80, one launch (start us, length us, event | category | flops | bytes accessed | tf_op | source)
XLA Modules:
  0.0 131.8 jit_solution(7774370649776657695)
XLA Ops:
  0.0 130.2 %shard_map.46 = f32[2,2,4,16,32]{4,3,2,1,0:T(8,128)} custom-call(s32[32]{0:T(128)} %group_hbm.1, s32[32]{0:T(128)} %ids_hbm.1, f32[2,1536,128]{2,1,0:T(8,128)} %bitcast.15, f32[32,2,48,128]{3,2,1,0:T(8,128)} %bitcast.16), custom_call_target="tpu_custom_call" | custom-call | tf_op jit(solution)/shard_map/pallas_call | solution.py:396
  130.2 1.6 %copy.8 = f32[2,2,4,32,16]{3,4,2,1,0:T(8,128)} copy(f32[2,2,4,32,16]{3,4,2,1,0:T(8,128)} %bitcast.17) | data formatting | bytes 65536

commit v6 on v5

--- a/solution.py
+++ b/solution.py
@@ -10,7 +10,7 @@
 MESH = pl.DeviceIdType.MESH
 LANES = 128
 Q = 2
-EARLY = 9
+EARLY = 8
 LATE = 0
 RELAYS = 4
 BEFORE = 3

time: 132 us -> 130 us (0.985)
  Pallas kernels: 130 us -> 128 us
    pallas_call x1, Pallas kernels: 130 us -> 128 us  [local(): pl.pallas_call(functools.partial(kernel, sizes), out_shape=jax.ShapeDtype...]
where the time goes in v6:
time: 130 us
  Pallas kernels  128 us (98%)
  local copies, waits for them, and re-layouts  1.57 us (1%)
    pallas_call x1, Pallas kernels, local(): pl.pallas_call(functools.partial(kernel, sizes), out_shape=jax.ShapeDtype...  128 us

profile of v6, /device:TPU:80, one launch (start us, length us, event | category | flops | bytes accessed | tf_op | source)
XLA Modules:
  0.0 129.7 jit_solution(4273047240487658128)
XLA Ops:
  0.0 128.1 %shard_map.46 = f32[2,2,4,16,32]{4,3,2,1,0:T(8,128)} custom-call(s32[32]{0:T(128)} %group_hbm.1, s32[32]{0:T(128)} %ids_hbm.1, f32[2,1536,128]{2,1,0:T(8,128)} %bitcast.15, f32[32,2,48,128]{3,2,1,0:T(8,128)} %bitcast.16), custom_call_target="tpu_custom_call" | custom-call | tf_op jit(solution)/shard_map/pallas_call | solution.py:396
  128.1 1.6 %copy.8 = f32[2,2,4,32,16]{3,4,2,1,0:T(8,128)} copy(f32[2,2,4,32,16]{3,4,2,1,0:T(8,128)} %bitcast.17) | data formatting | bytes 65536
